TPU v7x, 32 devices: a whole 2x2x4 slice. The times are simulated.
32 devices in a mesh: tok: 8 (over y, x, core), blk: 4 (over z).
Axes of the slice: x: 2, y: 2, z: 4, core: 2. Of those that a mesh axis runs over, the one named last changes fastest.
Arguments:
- activations: bfloat16 [4096, 4096], P('tok', 'blk'), may hold values from -52 to 52, as said below
- out_grads: bfloat16 [4096, 4096], P('tok', 'blk'), may hold values from -52 to 52, as said below
Outputs:
- act_inverse: float32 [4096, 4096], P(('tok', 'blk'))
- grad_inverse: float32 [4096, 4096], P(('tok', 'blk'))
Inputs may be any that keep to these rules, and one draw needn't show every extreme that they name: `activations`: real entries. `out_grads`: real entries.
All inputs are finite; a program needn't handle non-finite values.
Results may differ from a plain program's by a relative error of at most 0.02.
Values may be sent and summed in bfloat16 or wider, within the bound.
A program may use at most 64 MiB of HBM per device.

v0:
```python
import jax
import jax.numpy as jnp
from jax import lax
from jax.sharding import PartitionSpec as P

D = 4096
damping = 0.3
epsilon = 1e-06
divisor = 2.0


def column_squares(data):
    values = data.astype(jnp.float32)
    return jnp.sum(values * values, axis=0)


def fold_product(row_block, tile):
    return jnp.dot(
        row_block,
        lax.all_gather(tile, "tok", axis=0, tiled=True),
        preferred_element_type=jnp.float32,
    )


def newton_steps(scaled, identity):
    half = scaled.astype(jnp.bfloat16)
    row_block = lax.all_gather(half, "blk", axis=1, tiled=True)
    square = fold_product(row_block, half)
    cube = fold_product(row_block, square.astype(jnp.bfloat16))
    return 4.0 * identity - 6.0 * scaled + 4.0 * square - cube


def body(activations, out_grads):
    tok_count = lax.axis_size("tok")
    blk_count = lax.axis_size("blk")
    tok_id = lax.axis_index("tok")
    blk_id = lax.axis_index("blk")
    token_count = activations.shape[0] * tok_count
    tile_rows = D // tok_count
    tile_cols = D // blk_count
    full_acts, full_grads = (
        lax.all_gather(activations, "blk", axis=1, tiled=True),
        lax.all_gather(out_grads, "blk", axis=1, tiled=True),
    )
    sums_act, sums_grad = (
        lax.psum(column_squares(full_acts).astype(jnp.bfloat16), "tok").astype(jnp.float32),
        lax.psum(column_squares(full_grads).astype(jnp.bfloat16), "tok").astype(jnp.float32),
    )
    row_ids = tok_id * tile_rows + jnp.arange(tile_rows, dtype=jnp.int32)
    col_ids = blk_id * tile_cols + jnp.arange(tile_cols, dtype=jnp.int32)
    identity = (row_ids[:, None] == col_ids[None, :]).astype(jnp.float32)

    def damped_tile(full, local, sums):
        gram_tile = lax.psum_scatter(
            lax.dot_general(
                full, local, (((0,), (0,)), ((), ())), preferred_element_type=jnp.float32
            ).astype(jnp.bfloat16),
            "tok",
            scatter_dimension=0,
            tiled=True,
        ).astype(jnp.float32)
        inverse = lax.rsqrt(sums / token_count + epsilon)
        inverse_rows = lax.dynamic_slice_in_dim(inverse, tok_id * tile_rows, tile_rows)
        inverse_cols = lax.dynamic_slice_in_dim(inverse, blk_id * tile_cols, tile_cols)
        return (
            gram_tile / token_count * inverse_rows[:, None] * inverse_cols[None, :]
            + damping * identity
        )

    damped_act = damped_tile(full_acts, activations, sums_act)
    damped_grad = damped_tile(full_grads, out_grads, sums_grad)
    results = []
    for damped in (damped_act, damped_grad):
        scaled = damped / divisor
        result_tile = newton_steps(scaled, identity)
        results.append(
            lax.all_to_all(
                result_tile.astype(jnp.bfloat16), "blk", split_axis=0, concat_axis=1, tiled=True
            ).astype(result_tile.dtype)
        )
    return (results[0], results[1])


def solution(mesh):
    placed = (P("tok", "blk"), P("tok", "blk"))
    return jax.shard_map(
        body,
        mesh=mesh,
        in_specs=placed,
        out_specs=(P(("tok", "blk"), None), P(("tok", "blk"), None)),
        check_vma=False,
    )
```

profile of v0, /device:TPU:0, one launch (start us, length us, event | category | flops | bytes accessed | tf_op | source)
XLA Modules:
  0.0 763.5 jit_solution(1316433522095304969)
XLA Ops:
  8.7 84.3 %all-gather.9.cloned.1.call-done = bf16[512,4096]{1,0:T(8,128)(2,1)} async-done(((bf16[512,1024]{1,0:T(8,128)(2,1)}), bf16[512,4096]{1,0:T(8,128)(2,1)}) %all-gather.9.cloned.1.call-update) | async-done | bytes 4194320 | tf_op jit(solution)/shard_map/all_gather | solution.py:42
  93.0 9.1 %convolution_convert_fusion.1 = bf16[4096,1024]{1,0:T(8,128)(2,1)} fusion(bf16[512,4096]{1,0:T(8,128)(2,1)} %all-gather.9.cloned.1.call-done, bf16[512,1024]{1,0:T(8,128)(2,1)S(1)} %copy-done.1), kind=kOutput, calls=%fused_computation.3 | convolution fusion | flops 4299161600 | bytes 13631488 | tf_op jit(solution)/shard_map/dot_general | solution.py:55
  102.2 71.7 %all-gather.17.cloned.1.call-done = bf16[512,4096]{1,0:T(8,128)(2,1)} async-done(((bf16[512,1024]{1,0:T(8,128)(2,1)}), bf16[512,4096]{1,0:T(8,128)(2,1)}) %all-gather.17.cloned.1.call-update) | async-done | bytes 4194320 | tf_op jit(solution)/shard_map/all_gather | solution.py:43
  173.9 9.0 %convolution_convert_fusion = bf16[4096,1024]{1,0:T(8,128)(2,1)} fusion(bf16[512,4096]{1,0:T(8,128)(2,1)} %all-gather.17.cloned.1.call-done, bf16[512,1024]{1,0:T(8,128)(2,1)S(1)} %copy-done.2), kind=kOutput, calls=%fused_computation.2 | convolution fusion | flops 4299161600 | bytes 13631488 | tf_op jit(solution)/shard_map/dot_general | solution.py:55
  183.0 4.2 multiply_reduce_fusion
  189.1 24.5 %all-reduce = (bf16[4096]{0:T(1024)(128)(2,1)S(1)}, bf16[4096]{0:T(1024)(128)(2,1)S(1)}) all-reduce(bf16[4096]{0:T(1024)(128)(2,1)S(1)} %multiply_reduce_fusion.1, bf16[4096]{0:T(1024)(128)(2,1)S(1)} %multiply_reduce_fusion), channel_id=1, replica_groups=mesh['tok'=8,'blk'=4] {'tok'}, use_global_device_ids=true, to_apply=%region_2.0 | all-reduce | flops 8192 | bytes 32768 | tf_op jit(solution)/shard_map/psum | solution.py:46
  213.8 33.8 %reduce-scatter.3.cloned.1.call-done = bf16[512,1024]{1,0:T(8,128)(2,1)} async-done(((bf16[4096,1024]{1,0:T(8,128)(2,1)}), bf16[512,1024]{1,0:T(8,128)(2,1)}) %reduce-scatter.3.cloned.1.call-update) | async-done | bytes 1048592 | tf_op jit(solution)/shard_map/reduce_scatter | solution.py:54
  247.6 74.8 %reduce-scatter.5.cloned.1.call-done = bf16[512,1024]{1,0:T(8,128)(2,1)} async-done(((bf16[4096,1024]{1,0:T(8,128)(2,1)}), bf16[512,1024]{1,0:T(8,128)(2,1)}) %reduce-scatter.5.cloned.1.call-update) | async-done | bytes 1048592 | tf_op jit(solution)/shard_map/reduce_scatter | solution.py:54
  322.4 3.8 multiply_convert_fusion
  328.4 78.8 %all-gather.19.cloned.1.call-done = bf16[512,4096]{1,0:T(8,128)(2,1)} async-done(((bf16[512,1024]{1,0:T(8,128)(2,1)}), bf16[512,4096]{1,0:T(8,128)(2,1)}) %all-gather.19.cloned.1.call-update) | async-done | bytes 4194320 | tf_op jit(solution)/shard_map/all_gather | solution.py:27
  407.1 55.1 %all-gather.21.cloned.1.call-done = bf16[4096,1024]{1,0:T(8,128)(2,1)} async-done(((bf16[512,1024]{1,0:T(8,128)(2,1)}), bf16[4096,1024]{1,0:T(8,128)(2,1)}) %all-gather.21.cloned.1.call-update) | async-done | bytes 8388624 | tf_op jit(solution)/shard_map/all_gather | solution.py:20
  462.2 10.1 %fusion.9 = (bf16[512,1024]{1,0:T(8,128)(2,1)}, f32[512,1024]{1,0:T(8,128)S(1)}) fusion(bf16[512,4096]{1,0:T(8,128)(2,1)} %all-gather.19.cloned.1.call-done, bf16[4096,1024]{1,0:T(8,128)(2,1)} %all-gather.21.cloned.1.call-done), kind=kOutput, calls=%fused_computation.26 | convolution fusion | flops 4295491584 | bytes 15728640 | tf_op jit(solution)/shard_map/dot_general | solution.py:18
  472.6 72.5 %all-gather.11.cloned.1.call-done = bf16[512,4096]{1,0:T(8,128)(2,1)} async-done(((bf16[512,1024]{1,0:T(8,128)(2,1)}), bf16[512,4096]{1,0:T(8,128)(2,1)}) %all-gather.11.cloned.1.call-update) | async-done | bytes 4194320 | tf_op jit(solution)/shard_map/all_gather | solution.py:27
  545.1 55.2 %all-gather.13.cloned.1.call-done = bf16[4096,1024]{1,0:T(8,128)(2,1)} async-done(((bf16[512,1024]{1,0:T(8,128)(2,1)}), bf16[4096,1024]{1,0:T(8,128)(2,1)}) %all-gather.13.cloned.1.call-update) | async-done | bytes 8388624 | tf_op jit(solution)/shard_map/all_gather | solution.py:20
  600.4 10.8 %fusion.8 = (bf16[512,1024]{1,0:T(8,128)(2,1)}, f32[512,1024]{1,0:T(8,128)}) fusion(bf16[512,4096]{1,0:T(8,128)(2,1)} %all-gather.11.cloned.1.call-done, bf16[4096,1024]{1,0:T(8,128)(2,1)} %all-gather.13.cloned.1.call-done), kind=kOutput, calls=%fused_computation.25 | convolution fusion | flops 4295491584 | bytes 15728640 | tf_op jit(solution)/shard_map/dot_general | solution.py:18
  611.2 45.4 %all-gather.23.cloned.1.call-done = bf16[4096,1024]{1,0:T(8,128)(2,1)} async-done(((bf16[512,1024]{1,0:T(8,128)(2,1)}), bf16[4096,1024]{1,0:T(8,128)(2,1)}) %all-gather.23.cloned.1.call-update) | async-done | bytes 8388624 | tf_op jit(solution)/shard_map/all_gather | solution.py:20
  656.6 10.6 %fusion.7 = bf16[512,1024]{1,0:T(8,128)(2,1)} fusion(f32[512,1024]{1,0:T(8,128)S(1)} %get-tuple-element.9, bf16[512,1024]{1,0:T(8,128)(2,1)S(1)} %copy-done.4, bf16[512,4096]{1,0:T(8,128)(2,1)} %all-gather.19.cloned.1.call-done, bf16[4096,1024]{1,0:T(8,128)(2,1)} %all-gather.23.cloned.1.call-done, f32[1024]{0:T(1024)S(1)} %dynamic_slice.15, ...), kind=kOutput, calls=%fused_computation.14 | convolution fusion | flops 4301783040 | bytes 16789504 | tf_op jit(solution)/shard_map/dot_general | solution.py:18
  667.2 4.7 all-to-all-start.1
  671.9 41.2 %all-gather.15.cloned.1.call-done = bf16[4096,1024]{1,0:T(8,128)(2,1)} async-done(((bf16[512,1024]{1,0:T(8,128)(2,1)}), bf16[4096,1024]{1,0:T(8,128)(2,1)}) %all-gather.15.cloned.1.call-update) | async-done | bytes 8388624 | tf_op jit(solution)/shard_map/all_gather | solution.py:20
  713.2 11.1 %fusion.4 = bf16[512,1024]{1,0:T(8,128)(2,1)} fusion(f32[512,1024]{1,0:T(8,128)} %get-tuple-element.7, bf16[512,1024]{1,0:T(8,128)(2,1)S(1)} %copy-done.3, bf16[512,4096]{1,0:T(8,128)(2,1)} %all-gather.11.cloned.1.call-done, bf16[4096,1024]{1,0:T(8,128)(2,1)} %all-gather.15.cloned.1.call-done, f32[1024]{0:T(1024)S(1)} %dynamic_slice.13, ...), kind=kOutput, calls=%fused_computation.11 | convolution fusion | flops 4301783040 | bytes 16789504 | tf_op jit(solution)/shard_map/dot_general | solution.py:18
  724.3 4.6 all-to-all-start
  729.1 1.5 copy.7
  730.6 24.4 %all-to-all-done = bf16[4,128,1024]{2,1,0:T(8,128)(2,1)S(1)} async-done(((bf16[4,128,1024]{2,1,0:T(8,128)(2,1)}), bf16[4,128,1024]{2,1,0:T(8,128)(2,1)S(1)}, u32[]{:S(2)}, u32[]{:S(2)}) %all-to-all-start) | async-done | bytes 1048608 | tf_op jit(solution)/shard_map/all_to_all | solution.py:77
  755.2 1.5 copy.6
  (41 shorter events, 6.6 us)
Async XLA Ops:
  7.2 85.9 %copy-start.1 = (bf16[512,1024]{1,0:T(8,128)(2,1)S(1)}, bf16[512,1024]{1,0:T(8,128)(2,1)}, u32[]{:S(2)}) copy-start(bf16[512,1024]{1,0:T(8,128)(2,1)} %param.2) | copy-start | bytes 3145732
  7.2 85.9 %all-gather.9.cloned.1.call-start = ((), (), s32[]{:S(2)}) async-start(), calls=%async_computation.4 | async-start | bytes 5242880 | tf_op jit(solution)/shard_map/all_gather | solution.py:42
  7.9 166.0 %all-gather.17.cloned.1.call-start = ((), (), s32[]{:S(2)}) async-start(), calls=%async_computation.9 | async-start | bytes 5242880 | tf_op jit(solution)/shard_map/all_gather | solution.py:43
  8.7 238.9 %reduce-scatter.3.cloned.1.call-start = ((), (), s32[]{:S(2)}) async-start(), calls=%async_computation.5 | async-start | bytes 9437184 | tf_op jit(solution)/shard_map/reduce_scatter | solution.py:54
  102.1 71.7 %copy-start.2 = (bf16[512,1024]{1,0:T(8,128)(2,1)S(1)}, bf16[512,1024]{1,0:T(8,128)(2,1)}, u32[]{:S(2)}) copy-start(bf16[512,1024]{1,0:T(8,128)(2,1)} %param.3) | copy-start | bytes 3145732
  102.2 220.2 %reduce-scatter.5.cloned.1.call-start = ((), (), s32[]{:S(2)}) async-start(), calls=%async_computation.10 | async-start | bytes 9437184 | tf_op jit(solution)/shard_map/reduce_scatter | solution.py:54
  182.9 224.3 %all-gather.19.cloned.1.call-start = ((), (), s32[]{:S(2)}) async-start(), calls=%async_computation.11 | async-start | bytes 5242880 | tf_op jit(solution)/shard_map/all_gather | solution.py:27
  183.0 5.2 copy-start
  326.2 136.0 %all-gather.21.cloned.1.call-start = ((), (), s32[]{:S(2)}) async-start(), calls=%async_computation.12 | async-start | bytes 9437184 | tf_op jit(solution)/shard_map/all_gather | solution.py:20
  326.8 218.3 %all-gather.11.cloned.1.call-start = ((), (), s32[]{:S(2)}) async-start(), calls=%async_computation.6 | async-start | bytes 5242880 | tf_op jit(solution)/shard_map/all_gather | solution.py:27
  327.6 272.8 %all-gather.13.cloned.1.call-start = ((), (), s32[]{:S(2)}) async-start(), calls=%async_computation.7 | async-start | bytes 9437184 | tf_op jit(solution)/shard_map/all_gather | solution.py:20
  328.3 328.3 %all-gather.23.cloned.1.call-start = ((), (), s32[]{:S(2)}) async-start(), calls=%async_computation.13 | async-start | bytes 9437184 | tf_op jit(solution)/shard_map/all_gather | solution.py:20
  472.4 184.2 %copy-start.4 = (bf16[512,1024]{1,0:T(8,128)(2,1)S(1)}, bf16[512,1024]{1,0:T(8,128)(2,1)}, u32[]{:S(2)}) copy-start(bf16[512,1024]{1,0:T(8,128)(2,1)} %reduce-scatter.5.cloned.1.call-done) | copy-start | bytes 3145732
  472.4 240.8 %all-gather.15.cloned.1.call-start = ((), (), s32[]{:S(2)}) async-start(), calls=%async_computation.8 | async-start | bytes 9437184 | tf_op jit(solution)/shard_map/all_gather | solution.py:20
  667.2 46.0 %copy-start.3 = (bf16[512,1024]{1,0:T(8,128)(2,1)S(1)}, bf16[512,1024]{1,0:T(8,128)(2,1)}, u32[]{:S(2)}) copy-start(bf16[512,1024]{1,0:T(8,128)(2,1)} %reduce-scatter.3.cloned.1.call-done) | copy-start | bytes 3145732
  667.2 57.0 %all-to-all-start.1 = ((bf16[4,128,1024]{2,1,0:T(8,128)(2,1)}), bf16[4,128,1024]{2,1,0:T(8,128)(2,1)S(1)}, u32[]{:S(2)}, u32[]{:S(2)}) async-start(bf16[4,128,1024]{2,1,0:T(8,128)(2,1)} %bitcast.2), calls=%async_computation.3 | async-start | bytes 2097152 | tf_op jit(solution)/shard_map/all_to_all | solution.py:77
  724.3 30.7 %all-to-all-start = ((bf16[4,128,1024]{2,1,0:T(8,128)(2,1)}), bf16[4,128,1024]{2,1,0:T(8,128)(2,1)S(1)}, u32[]{:S(2)}, u32[]{:S(2)}) async-start(bf16[4,128,1024]{2,1,0:T(8,128)(2,1)} %bitcast), calls=%async_computation.1 | async-start | bytes 2097152 | tf_op jit(solution)/shard_map/all_to_all | solution.py:77
Sparse Core Ops, SparseCore 0:
  9.6 83.4 all-gather.8
  94.6 79.2 all-gather.16
  177.3 70.1 reduce-scatter.2
  250.9 71.4 reduce-scatter.4
  326.4 80.7 all-gather.18
  409.5 52.7 all-gather.20
  464.4 80.7 all-gather.10
  547.6 52.7 all-gather.12
  602.3 54.2 all-gather.22
  658.9 54.2 all-gather.14
where the time goes:
time: 764 us
  waiting for transfers between devices  641 us (84%)
  matrix products  60.7 us (8%)
  blocking collectives  24.5 us (3%)
  between operations  14.3 us (2%)
  starting transfers between devices  9.9 us (1%)
  other arithmetic  9.53 us (1%)
    all_gather x4, waiting for transfers between devices, fold_product(): lax.all_gather(tile, 'tok', axis=0, tiled=True)  197 us
    all_gather x2, waiting for transfers between devices, newton_steps(): row_block = lax.all_gather(half, 'blk', axis=1, tiled=True)  151 us
    reduce_scatter x2, waiting for transfers between devices, damped_tile(): lax.psum_scatter(lax.dot_general(full, local, (((0,), (0,)), ((), ())), p...  109 us
    all_gather x1, waiting for transfers between devices, body(): lax.all_gather(activations, 'blk', axis=1, tiled=True)  84.3 us
    all_gather x1, waiting for transfers between devices, body(): lax.all_gather(out_grads, 'blk', axis=1, tiled=True)  71.7 us
    dot_general x4, matrix products, fold_product(): jnp.dot(row_block, lax.all_gather(tile, 'tok', axis=0, tiled=True), prefe...  42.6 us
    psum x1, blocking collectives, body(): lax.psum(column_squares(full_acts).astype(jnp.bfloat16), 'tok')  24.5 us
    all_to_all x2, waiting for transfers between devices, body(): lax.all_to_all(result_tile.astype(jnp.bfloat16), 'blk', split_axis=0, con...  24.4 us
  transfers between devices with their start and end apart: 12, of which 11 were waited for; matrix products, arithmetic and copies ran while one was open for 9% of the time, Pallas kernels for 0%

commit v1 on v0

--- a/solution.py
+++ b/solution.py
@@ -24,7 +24,12 @@
 
 def newton_steps(scaled, identity):
     half = scaled.astype(jnp.bfloat16)
-    row_block = lax.all_gather(half, "blk", axis=1, tiled=True)
+    ring = [half]
+    for hop in range(3):
+        ring.append(lax.ppermute(ring[-1], "blk", [(dev, (dev + 1) % 4) for dev in range(4)]))
+    row_block = jnp.roll(
+        jnp.concatenate(ring[::-1], axis=1), (lax.axis_index("blk") + 1) * ring[0].shape[1], axis=1
+    )
     square = fold_product(row_block, half)
     cube = fold_product(row_block, square.astype(jnp.bfloat16))
     return 4.0 * identity - 6.0 * scaled + 4.0 * square - cube

time: 764 us -> 619 us (0.81)
  waiting for transfers between devices: 641 us -> 475 us
  other arithmetic: 9.53 us -> 26.8 us
    all_gather x4, waiting for transfers between devices: 197 us -> 36.3 us  [fold_product(): lax.all_gather(tile, 'tok', axis=0, tiled=True)]
    all_gather x2 -> x0, waiting for transfers between devices: 151 us -> none  [newton_steps(): row_block = lax.all_gather(half, 'blk', axis=1, tiled=True)]
    ppermute x0 -> x6, waiting for transfers between devices: none -> 149 us  [newton_steps(): lax.ppermute(ring[-1], 'blk', [(dev, (dev + 1) % 4) for dev in range(4)])]
    concatenate x0 -> x2, other arithmetic: none -> 17.2 us  [newton_steps(): jnp.roll(jnp.concatenate(ring[::-1], axis=1), (lax.axis_index('blk') + 1)...]
    all_gather x1, waiting for transfers between devices: 84.3 us -> 70.2 us  [body(): lax.all_gather(activations, 'blk', axis=1, tiled=True)]
    all_gather x1, waiting for transfers between devices: 71.7 us -> 84.3 us  [body(): lax.all_gather(out_grads, 'blk', axis=1, tiled=True)]
  transfers between devices with their start and end apart: 12 -> 16, of which waited for: 11 -> 12; matrix products, arithmetic and copies ran while one was open for 9% -> 14% of each run, Pallas kernels for 0% -> 0%
where the time goes in v1:
time: 619 us
  waiting for transfers between devices  475 us (77%)
  matrix products  64.1 us (10%)
  other arithmetic  26.8 us (4%)
  blocking collectives  24.5 us (4%)
  between operations  14.3 us (2%)
  starting transfers between devices  10.3 us (2%)
    ppermute x6, waiting for transfers between devices, newton_steps(): lax.ppermute(ring[-1], 'blk', [(dev, (dev + 1) % 4) for dev in range(4)])  149 us
    reduce_scatter x2, waiting for transfers between devices, damped_tile(): lax.psum_scatter(lax.dot_general(full, local, (((0,), (0,)), ((), ())), p...  109 us
    all_gather x1, waiting for transfers between devices, body(): lax.all_gather(out_grads, 'blk', axis=1, tiled=True)  84.3 us
    all_gather x1, waiting for transfers between devices, body(): lax.all_gather(activations, 'blk', axis=1, tiled=True)  70.2 us
    dot_general x4, matrix products, fold_product(): jnp.dot(row_block, lax.all_gather(tile, 'tok', axis=0, tiled=True), prefe...  44.6 us
    all_gather x4, waiting for transfers between devices, fold_product(): lax.all_gather(tile, 'tok', axis=0, tiled=True)  36.3 us
    psum x1, blocking collectives, body(): lax.psum(column_squares(full_acts).astype(jnp.bfloat16), 'tok')  24.5 us
    all_to_all x2, waiting for transfers between devices, body(): lax.all_to_all(result_tile.astype(jnp.bfloat16), 'blk', split_axis=0, con...  24.4 us
  transfers between devices with their start and end apart: 16, of which 12 were waited for; matrix products, arithmetic and copies ran while one was open for 14% of the time, Pallas kernels for 0%

profile of v1, /device:TPU:0, one launch (start us, length us, event | category | flops | bytes accessed | tf_op | source)
XLA Modules:
  0.0 618.8 jit_solution(11465068782064229488)
XLA Ops:
  8.7 84.3 %all-gather.13.cloned.1.call-done = bf16[512,4096]{1,0:T(8,128)(2,1)} async-done(((bf16[512,1024]{1,0:T(8,128)(2,1)}), bf16[512,4096]{1,0:T(8,128)(2,1)}) %all-gather.13.cloned.1.call-update) | async-done | bytes 4194320 | tf_op jit(solution)/shard_map/all_gather | solution.py:48
  93.0 10.5 %convolution_convert_fusion = bf16[4096,1024]{1,0:T(8,128)(2,1)} fusion(bf16[512,4096]{1,0:T(8,128)(2,1)} %all-gather.13.cloned.1.call-done, bf16[512,1024]{1,0:T(8,128)(2,1)} %param.5), kind=kOutput, calls=%fused_computation.18 | convolution fusion | flops 4299161600 | bytes 13631488 | tf_op jit(solution)/shard_map/dot_general | solution.py:60
  103.6 70.2 %all-gather.7.cloned.1.call-done = bf16[512,4096]{1,0:T(8,128)(2,1)} async-done(((bf16[512,1024]{1,0:T(8,128)(2,1)}), bf16[512,4096]{1,0:T(8,128)(2,1)}) %all-gather.7.cloned.1.call-update) | async-done | bytes 4194320 | tf_op jit(solution)/shard_map/all_gather | solution.py:47
  173.9 9.0 %convolution_convert_fusion.1 = bf16[4096,1024]{1,0:T(8,128)(2,1)} fusion(bf16[512,4096]{1,0:T(8,128)(2,1)} %all-gather.7.cloned.1.call-done, bf16[512,1024]{1,0:T(8,128)(2,1)S(1)} %copy-done.2), kind=kOutput, calls=%fused_computation.19 | convolution fusion | flops 4299161600 | bytes 13631488 | tf_op jit(solution)/shard_map/dot_general | solution.py:60
  183.0 4.2 multiply_reduce_fusion.1
  189.0 24.5 %all-reduce = (bf16[4096]{0:T(1024)(128)(2,1)S(1)}, bf16[4096]{0:T(1024)(128)(2,1)S(1)}) all-reduce(bf16[4096]{0:T(1024)(128)(2,1)S(1)} %multiply_reduce_fusion.1, bf16[4096]{0:T(1024)(128)(2,1)S(1)} %multiply_reduce_fusion), channel_id=1, replica_groups=mesh['tok'=8,'blk'=4] {'tok'}, use_global_device_ids=true, to_apply=%region_2.0 | all-reduce | flops 8192 | bytes 32768 | tf_op jit(solution)/shard_map/psum | solution.py:51
  213.7 33.8 %reduce-scatter.5.cloned.1.call-done = bf16[512,1024]{1,0:T(8,128)(2,1)} async-done(((bf16[4096,1024]{1,0:T(8,128)(2,1)}), bf16[512,1024]{1,0:T(8,128)(2,1)}) %reduce-scatter.5.cloned.1.call-update) | async-done | bytes 1048592 | tf_op jit(solution)/shard_map/reduce_scatter | solution.py:59
  247.5 74.8 %reduce-scatter.3.cloned.1.call-done = bf16[512,1024]{1,0:T(8,128)(2,1)} async-done(((bf16[4096,1024]{1,0:T(8,128)(2,1)}), bf16[512,1024]{1,0:T(8,128)(2,1)}) %reduce-scatter.3.cloned.1.call-update) | async-done | bytes 1048592 | tf_op jit(solution)/shard_map/reduce_scatter | solution.py:59
  322.4 3.8 multiply_convert_fusion
  328.4 25.3 %collective-permute-done = bf16[512,1024]{1,0:T(8,128)(2,1)S(1)} collective-permute-done((bf16[512,1024]{1,0:T(8,128)(2,1)}, bf16[512,1024]{1,0:T(8,128)(2,1)S(1)}, u32[]{:S(2)}, u32[]{:S(2)}) %collective-permute-start) | collective-permute-done | bytes 1048608 | tf_op jit(solution)/shard_map/ppermute | solution.py:29
  353.6 25.7 %collective-permute-done.1 = bf16[512,1024]{1,0:T(8,128)(2,1)S(1)} collective-permute-done((bf16[512,1024]{1,0:T(8,128)(2,1)S(1)}, bf16[512,1024]{1,0:T(8,128)(2,1)S(1)}, u32[]{:S(2)}, u32[]{:S(2)}) %collective-permute-start.1) | collective-permute-done | bytes 1048608 | tf_op jit(solution)/shard_map/ppermute | solution.py:29
  379.3 24.8 %collective-permute-done.2 = bf16[512,1024]{1,0:T(8,128)(2,1)S(1)} collective-permute-done((bf16[512,1024]{1,0:T(8,128)(2,1)S(1)}, bf16[512,1024]{1,0:T(8,128)(2,1)S(1)}, u32[]{:S(2)}, u32[]{:S(2)}) %collective-permute-start.2) | collective-permute-done | bytes 1048608 | tf_op jit(solution)/shard_map/ppermute | solution.py:29
  404.1 9.0 %fusion.10 = bf16[512,4096]{1,0:T(8,128)(2,1)} fusion(s32[]{:T(128)S(6)} %select_n.23, bf16[512,1024]{1,0:T(8,128)(2,1)S(1)} %collective-permute-done.2, bf16[512,1024]{1,0:T(8,128)(2,1)S(1)} %collective-permute-done.1, bf16[512,1024]{1,0:T(8,128)(2,1)S(1)} %collective-permute-done, bf16[512,1024]{1,0:T(8,128)(2,1)} %get-tuple-element.6), kind=kLoop, calls=%fused_computation.30 | loop fusion | flops 33554432 | bytes 8388612 | tf_op jit(solution)/shard_map/jit(_roll_dynamic)/concatenate | solution.py:30
  413.1 10.9 %fusion.22 = (bf16[512,1024]{1,0:T(8,128)(2,1)}, f32[512,1024]{1,0:T(8,128)}) fusion(bf16[512,4096]{1,0:T(8,128)(2,1)} %fusion.10, bf16[4096,1024]{1,0:T(8,128)(2,1)} %all-gather.9.cloned.1.call-done), kind=kOutput, calls=%fused_computation.55 | convolution fusion | flops 4295491584 | bytes 15728640 | tf_op jit(solution)/shard_map/dot_general | solution.py:18
  424.2 25.3 %collective-permute-done.3 = bf16[512,1024]{1,0:T(8,128)(2,1)S(1)} collective-permute-done((bf16[512,1024]{1,0:T(8,128)(2,1)S(1)}, bf16[512,1024]{1,0:T(8,128)(2,1)S(1)}, u32[]{:S(2)}, u32[]{:S(2)}) %collective-permute-start.3) | collective-permute-done | bytes 1048608 | tf_op jit(solution)/shard_map/ppermute | solution.py:29
  449.5 24.4 %collective-permute-done.4 = bf16[512,1024]{1,0:T(8,128)(2,1)S(1)} collective-permute-done((bf16[512,1024]{1,0:T(8,128)(2,1)S(1)}, bf16[512,1024]{1,0:T(8,128)(2,1)S(1)}, u32[]{:S(2)}, u32[]{:S(2)}) %collective-permute-start.4) | collective-permute-done | bytes 1048608 | tf_op jit(solution)/shard_map/ppermute | solution.py:29
  473.9 23.6 %collective-permute-done.5 = bf16[512,1024]{1,0:T(8,128)(2,1)S(1)} collective-permute-done((bf16[512,1024]{1,0:T(8,128)(2,1)S(1)}, bf16[512,1024]{1,0:T(8,128)(2,1)S(1)}, u32[]{:S(2)}, u32[]{:S(2)}) %collective-permute-start.5) | collective-permute-done | bytes 1048608 | tf_op jit(solution)/shard_map/ppermute | solution.py:29
  497.5 8.2 %fusion.3 = bf16[512,4096]{1,0:T(8,128)(2,1)} fusion(s32[]{:T(128)S(6)} %select_n.23, bf16[512,1024]{1,0:T(8,128)(2,1)S(1)} %collective-permute-done.5, bf16[512,1024]{1,0:T(8,128)(2,1)S(1)} %collective-permute-done.4, bf16[512,1024]{1,0:T(8,128)(2,1)S(1)} %collective-permute-done.3, bf16[512,1024]{1,0:T(8,128)(2,1)S(1)} %copy-done), kind=kLoop, calls=%fused_computation.23 | loop fusion | flops 33554432 | bytes 8388612 | tf_op jit(solution)/shard_map/jit(_roll_dynamic)/concatenate | solution.py:30
  505.7 10.9 %fusion.23 = (bf16[512,1024]{1,0:T(8,128)(2,1)}, f32[512,1024]{1,0:T(8,128)}) fusion(bf16[512,4096]{1,0:T(8,128)(2,1)} %fusion.3, bf16[4096,1024]{1,0:T(8,128)(2,1)} %all-gather.15.cloned.1.call-done), kind=kOutput, calls=%fused_computation.56 | convolution fusion | flops 4295491584 | bytes 15728640 | tf_op jit(solution)/shard_map/dot_general | solution.py:18
  516.7 11.7 %fusion.18 = bf16[512,1024]{1,0:T(8,128)(2,1)} fusion(f32[512,1024]{1,0:T(8,128)} %get-tuple-element.8, bf16[512,1024]{1,0:T(8,128)(2,1)S(1)} %copy-done.4, bf16[512,4096]{1,0:T(8,128)(2,1)} %fusion.10, bf16[4096,1024]{1,0:T(8,128)(2,1)} %all-gather.11.cloned.1.call-done, f32[1024]{0:T(1024)S(1)} %dynamic_slice.16, ...), kind=kOutput, calls=%fused_computation.41 | convolution fusion | flops 4301783040 | bytes 16789504 | tf_op jit(solution)/shard_map/dot_general | solution.py:18
  532.2 36.3 %all-gather.17.cloned.1.call-done = bf16[4096,1024]{1,0:T(8,128)(2,1)} async-done(((bf16[512,1024]{1,0:T(8,128)(2,1)}), bf16[4096,1024]{1,0:T(8,128)(2,1)}) %all-gather.17.cloned.1.call-update) | async-done | bytes 8388624 | tf_op jit(solution)/shard_map/all_gather | solution.py:20
  568.5 11.1 %fusion.21 = bf16[512,1024]{1,0:T(8,128)(2,1)} fusion(f32[512,1024]{1,0:T(8,128)} %get-tuple-element.10, bf16[512,1024]{1,0:T(8,128)(2,1)S(1)} %copy-done.3, bf16[512,4096]{1,0:T(8,128)(2,1)} %fusion.3, bf16[4096,1024]{1,0:T(8,128)(2,1)} %all-gather.17.cloned.1.call-done, f32[1024]{0:T(1024)S(1)} %dynamic_slice.18, f32[512]{0:T(512)S(1)} %dynamic-slice_multiply_fusion, ...), kind=kOutput, calls=%fused_computation.44 | convolution fusion | flops 4301783040 | bytes 16789504 | tf_op jit(solution)/shard_map/dot_general | solution.py:18
  579.6 4.6 all-to-all-start.1
  585.9 24.4 %all-to-all-done.1 = bf16[4,128,1024]{2,1,0:T(8,128)(2,1)S(1)} async-done(((bf16[4,128,1024]{2,1,0:T(8,128)(2,1)}), bf16[4,128,1024]{2,1,0:T(8,128)(2,1)S(1)}, u32[]{:S(2)}, u32[]{:S(2)}) %all-to-all-start.1) | async-done | bytes 1048608 | tf_op jit(solution)/shard_map/all_to_all | solution.py:82
  (49 shorter events, 13.2 us)
Async XLA Ops:
  7.2 85.9 %all-gather.13.cloned.1.call-start = ((), (), s32[]{:S(2)}) async-start(), calls=%async_computation.8 | async-start | bytes 5242880 | tf_op jit(solution)/shard_map/all_gather | solution.py:48
  7.9 166.0 %all-gather.7.cloned.1.call-start = ((), (), s32[]{:S(2)}) async-start(), calls=%async_computation.4 | async-start | bytes 5242880 | tf_op jit(solution)/shard_map/all_gather | solution.py:47
  8.6 238.9 %reduce-scatter.5.cloned.1.call-start = ((), (), s32[]{:S(2)}) async-start(), calls=%async_computation.9 | async-start | bytes 9437184 | tf_op jit(solution)/shard_map/reduce_scatter | solution.py:59
  103.6 70.3 %copy-start.2 = (bf16[512,1024]{1,0:T(8,128)(2,1)S(1)}, bf16[512,1024]{1,0:T(8,128)(2,1)}, u32[]{:S(2)}) copy-start(bf16[512,1024]{1,0:T(8,128)(2,1)} %param.4) | copy-start | bytes 3145732
  103.6 218.8 %reduce-scatter.3.cloned.1.call-start = ((), (), s32[]{:S(2)}) async-start(), calls=%async_computation.5 | async-start | bytes 9437184 | tf_op jit(solution)/shard_map/reduce_scatter | solution.py:59
  182.9 230.3 %all-gather.9.cloned.1.call-start = ((), (), s32[]{:S(2)}) async-start(), calls=%async_computation.6 | async-start | bytes 9437184 | tf_op jit(solution)/shard_map/all_gather | solution.py:20
  182.9 5.2 copy-start.1
  326.2 179.5 %all-gather.15.cloned.1.call-start = ((), (), s32[]{:S(2)}) async-start(), calls=%async_computation.10 | async-start | bytes 9437184 | tf_op jit(solution)/shard_map/all_gather | solution.py:20
  326.8 189.8 %all-gather.11.cloned.1.call-start = ((), (), s32[]{:S(2)}) async-start(), calls=%async_computation.7 | async-start | bytes 9437184 | tf_op jit(solution)/shard_map/all_gather | solution.py:20
  326.8 26.8 %collective-permute-start = (bf16[512,1024]{1,0:T(8,128)(2,1)}, bf16[512,1024]{1,0:T(8,128)(2,1)S(1)}, u32[]{:S(2)}, u32[]{:S(2)}) collective-permute-start(bf16[512,1024]{1,0:T(8,128)(2,1)} %get-tuple-element.6), channel_id=1, source_target_pairs={{0,1},{1,2},{2,3},{3,0},{4,5},{5,6},{6,7},{7,4},{8,9},{9,10},{10,1... | collective-permute-start | bytes 3145736 | tf_op jit(solution)/shard_map/ppermute | solution.py:29
  353.6 25.7 %collective-permute-start.1 = (bf16[512,1024]{1,0:T(8,128)(2,1)S(1)}, bf16[512,1024]{1,0:T(8,128)(2,1)S(1)}, u32[]{:S(2)}, u32[]{:S(2)}) collective-permute-start(bf16[512,1024]{1,0:T(8,128)(2,1)S(1)} %collective-permute-done), channel_id=1, source_target_pairs={{0,1},{1,2},{2,3},{3,0},{4,5},{5,6},{6,7},{7,4},{8,9},{9,10},{10,1... | collective-permute-start | bytes 3145736 | tf_op jit(solution)/shard_map/ppermute | solution.py:29
  379.3 24.8 %collective-permute-start.2 = (bf16[512,1024]{1,0:T(8,128)(2,1)S(1)}, bf16[512,1024]{1,0:T(8,128)(2,1)S(1)}, u32[]{:S(2)}, u32[]{:S(2)}) collective-permute-start(bf16[512,1024]{1,0:T(8,128)(2,1)S(1)} %collective-permute-done.1), channel_id=1, source_target_pairs={{0,1},{1,2},{2,3},{3,0},{4,5},{5,6},{6,7},{7,4},{8,9},{9,10},{10,1... | collective-permute-start | bytes 3145736 | tf_op jit(solution)/shard_map/ppermute | solution.py:29
  413.1 11.0 %copy-start = (bf16[512,1024]{1,0:T(8,128)(2,1)S(1)}, bf16[512,1024]{1,0:T(8,128)(2,1)}, u32[]{:S(2)}) copy-start(bf16[512,1024]{1,0:T(8,128)(2,1)} %get-tuple-element.5) | copy-start | bytes 3145732
  424.1 144.4 %all-gather.17.cloned.1.call-start = ((), (), s32[]{:S(2)}) async-start(), calls=%async_computation.11 | async-start | bytes 9437184 | tf_op jit(solution)/shard_map/all_gather | solution.py:20
  424.2 25.3 %collective-permute-start.3 = (bf16[512,1024]{1,0:T(8,128)(2,1)S(1)}, bf16[512,1024]{1,0:T(8,128)(2,1)S(1)}, u32[]{:S(2)}, u32[]{:S(2)}) collective-permute-start(bf16[512,1024]{1,0:T(8,128)(2,1)S(1)} %copy-done), channel_id=1, source_target_pairs={{0,1},{1,2},{2,3},{3,0},{4,5},{5,6},{6,7},{7,4},{8,9},{9,10},{10,1... | collective-permute-start | bytes 3145736 | tf_op jit(solution)/shard_map/ppermute | solution.py:29
  449.5 24.4 %collective-permute-start.4 = (bf16[512,1024]{1,0:T(8,128)(2,1)S(1)}, bf16[512,1024]{1,0:T(8,128)(2,1)S(1)}, u32[]{:S(2)}, u32[]{:S(2)}) collective-permute-start(bf16[512,1024]{1,0:T(8,128)(2,1)S(1)} %collective-permute-done.3), channel_id=1, source_target_pairs={{0,1},{1,2},{2,3},{3,0},{4,5},{5,6},{6,7},{7,4},{8,9},{9,10},{10,1... | collective-permute-start | bytes 3145736 | tf_op jit(solution)/shard_map/ppermute | solution.py:29
  473.9 23.6 %collective-permute-start.5 = (bf16[512,1024]{1,0:T(8,128)(2,1)S(1)}, bf16[512,1024]{1,0:T(8,128)(2,1)S(1)}, u32[]{:S(2)}, u32[]{:S(2)}) collective-permute-start(bf16[512,1024]{1,0:T(8,128)(2,1)S(1)} %collective-permute-done.4), channel_id=1, source_target_pairs={{0,1},{1,2},{2,3},{3,0},{4,5},{5,6},{6,7},{7,4},{8,9},{9,10},{10,1... | collective-permute-start | bytes 3145736 | tf_op jit(solution)/shard_map/ppermute | solution.py:29
  505.7 10.9 %copy-start.4 = (bf16[512,1024]{1,0:T(8,128)(2,1)S(1)}, bf16[512,1024]{1,0:T(8,128)(2,1)}, u32[]{:S(2)}) copy-start(bf16[512,1024]{1,0:T(8,128)(2,1)} %reduce-scatter.3.cloned.1.call-done) | copy-start | bytes 3145732
  516.6 51.8 %copy-start.3 = (bf16[512,1024]{1,0:T(8,128)(2,1)S(1)}, bf16[512,1024]{1,0:T(8,128)(2,1)}, u32[]{:S(2)}) copy-start(bf16[512,1024]{1,0:T(8,128)(2,1)} %reduce-scatter.5.cloned.1.call-done) | copy-start | bytes 3145732
  528.4 51.2 %all-to-all-start = ((bf16[4,128,1024]{2,1,0:T(8,128)(2,1)}), bf16[4,128,1024]{2,1,0:T(8,128)(2,1)S(1)}, u32[]{:S(2)}, u32[]{:S(2)}) async-start(bf16[4,128,1024]{2,1,0:T(8,128)(2,1)} %bitcast), calls=%async_computation.1 | async-start | bytes 2097152 | tf_op jit(solution)/shard_map/all_to_all | solution.py:82
  579.6 30.7 %all-to-all-start.1 = ((bf16[4,128,1024]{2,1,0:T(8,128)(2,1)}), bf16[4,128,1024]{2,1,0:T(8,128)(2,1)S(1)}, u32[]{:S(2)}, u32[]{:S(2)}) async-start(bf16[4,128,1024]{2,1,0:T(8,128)(2,1)} %bitcast.2), calls=%async_computation.3 | async-start | bytes 2097152 | tf_op jit(solution)/shard_map/all_to_all | solution.py:82
Sparse Core Ops, SparseCore 0:
  9.5 83.4 all-gather.12
  94.6 79.2 all-gather.6
  177.3 70.1 reduce-scatter.4
  250.9 71.4 reduce-scatter.2
  326.3 54.2 all-gather.8
  383.0 54.2 all-gather.14
  439.1 54.2 all-gather.10
  516.7 51.6 all-gather.16
